TPU v7x, 32 devices: a whole 2x2x4 slice. The times are simulated.
32 devices in a mesh: dp: 8 (over y, x, core), expert: 4 (over z).
Axes of the slice: x: 2, y: 2, z: 4, core: 2. Of those that a mesh axis runs over, the one named last changes fastest.
Arguments:
- grad_out: bfloat16 [4, 2048, 1024], P(None, ('dp', 'expert')), may hold values from -12 to 12
- routes: int32 [4, 2048, 8], P(None, ('dp', 'expert')), may hold values from 0 to 127, all different within a row; in each aligned block of 64 rows (0 to 63, 64 to 127, ..., all dimensions but the last counted through in order) at most 8 rows name the same one
- route_probs: bfloat16 [4, 2048, 8], P(None, ('dp', 'expert')), may hold values from 0.049804688 to 0.3984375
- dispatched: bfloat16 [4, 1024, 1024], P(None, ('dp', 'expert')), may hold values from -12 to 12, as said below
- w_gate: bfloat16 [1024, 1024], P(None, 'expert'), may hold values from -0.1875 to 0.1875
- w_up: bfloat16 [1024, 1024], P(None, 'expert'), may hold values from -0.1875 to 0.1875
- w_down: bfloat16 [1024, 1024], P('expert'), may hold values from -0.25 to 0.25
Outputs:
- grad_in: bfloat16 [4, 2048, 1024], P(None, ('dp', 'expert'))
- grad_gate: float32 [1024, 1024], P('dp', 'expert')
- grad_up: float32 [1024, 1024], P('dp', 'expert')
- grad_down_t: float32 [1024, 1024], P('dp', 'expert')
Inputs may be any that keep to these rules, and one draw needn't show every extreme that they name: `routes`: in each micro-batch, among the 64 rows of one device no expert is named more than 8 times, a bound that some expert reaches in some of these blocks. `dispatched`: within each group of 4 consecutive blocks of 32 rows, blocks 2e and 2e + 1 are equal.
All inputs are finite; a program needn't handle non-finite values.
Results may differ from a plain program's by a relative error of at most 0.0058.
Values may be sent and summed in bfloat16 or wider, within the bound.
A program may use at most 64 MiB of HBM per device.

v0:
```python
import functools

import jax
import jax.numpy as jnp
from jax import lax
from jax.experimental import pallas as pl
from jax.experimental.pallas import tpu as pltpu
from jax.sharding import PartitionSpec as P

CAPS = 8
MESH = pl.DeviceIdType.MESH
BF16 = jnp.bfloat16
F32 = jnp.float32


def dot(left, right, lc, rc):
    return lax.dot_general(
        left, right, (((lc,), (rc,)), ((), ())), preferred_element_type=F32
    )


def flipped(index, bits):
    step = 1
    while step <= bits:
        if bits & step:
            index = index + step - 2 * step * lax.rem(lax.div(index, step), 2)
        step *= 2
    return index


def kernel(
    micro,
    n_exp,
    n_dp,
    routes_ref,
    probs_ref,
    go_hbm,
    x_hbm,
    wg_hbm,
    wu_hbm,
    wd_hbm,
    gin_ref,
    gg_ref,
    gu_ref,
    gd_ref,
    go_v,
    x_v,
    wg_v,
    wu_v,
    wd_v,
    a_send,
    a_buf,
    r_send,
    r_buf,
    acc,
    p1_send,
    p1_buf,
    p2_send,
    p2_buf,
    s_all,
    h_all,
    load_sem,
    a_ssem,
    a_rsem,
    r_ssem,
    r_rsem,
    p1_ssem,
    p1_rsem,
    p2_ssem,
    p2_rsem,
    s_ssem,
    s_rsem,
    h_ssem,
    h_rsem,
):
    member = lax.axis_index("expert")
    replica = lax.axis_index("dp")
    core = lax.rem(replica, 2)
    chip = lax.div(replica, 2)
    chips = n_dp // 2
    partner = {"dp": chip * 2 + 1 - core}
    window = n_exp // 2
    tokens = go_v.shape[0]
    width = go_v.shape[1]
    tok_dev = tokens // micro
    part = micro * CAPS
    rows = n_exp * part
    row_block = width // n_dp
    gather = row_block % 128 == 0

    def member_at(k):
        return flipped(member, k)

    def chip_at(k):
        return {"dp": flipped(chip, k) * 2 + core}

    loads = [
        pltpu.make_async_copy(src, dst, load_sem.at[i])
        for i, (src, dst) in enumerate(
            ((go_hbm, go_v), (x_hbm, x_v), (wg_hbm, wg_v), (wu_hbm, wu_v), (wd_hbm, wd_v))
        )
    ]
    for load in loads:
        load.start()

    barrier = pltpu.get_barrier_semaphore()
    for k in range(1, n_exp):
        pl.semaphore_signal(
            barrier, inc=1, device_id={"expert": member_at(k)}, device_id_type=MESH
        )
    for k in range(1, n_dp):
        pl.semaphore_signal(
            barrier, inc=1, device_id={"dp": flipped(replica, k)}, device_id_type=MESH
        )

    ids = jnp.concatenate([routes_ref[m] for m in range(micro)], axis=1)
    probs = jnp.concatenate([probs_ref[m].astype(F32) for m in range(micro)], axis=1)
    pad = max(window, 8)
    expert_row = lax.broadcasted_iota(jnp.int32, (pad, tokens), 0)
    hits, weights = [], []
    table = jnp.zeros((pad, tokens), F32)
    for e in range(window):
        named = ids == e
        hits.append(jnp.sum(jnp.where(named, 1.0, 0.0), axis=0, keepdims=True))
        weights.append(jnp.sum(jnp.where(named, probs, 0.0), axis=0, keepdims=True))
        table = jnp.where(expert_row == e, hits[e], table)
    ti = lax.broadcasted_iota(jnp.int32, (tokens, tokens), 0)
    tj = lax.broadcasted_iota(jnp.int32, (tokens, tokens), 1)
    earlier = jnp.where((ti < tj) & (lax.div(ti, tok_dev) == lax.div(tj, tok_dev)), 1.0, 0.0)
    ranking = dot(table.astype(BF16), earlier.astype(BF16), 1, 0)
    slot = lax.broadcasted_iota(jnp.int32, (CAPS, tokens), 0).astype(F32)
    batch = lax.div(lax.broadcasted_iota(jnp.int32, (CAPS, tokens), 1), tok_dev)
    ones, scales = [], []
    for h in range(n_exp):
        e = h // 2
        chosen = (hits[e] > 0.5) & (ranking[e : e + 1] == slot)
        for m in range(micro):
            here = chosen & (batch == m)
            ones.append(jnp.where(here, 1.0, 0.0))
            scales.append(jnp.where(here, weights[e], 0.0))
    mixing = jnp.concatenate(ones, axis=0).astype(BF16)
    picking = jnp.concatenate(scales, axis=0).astype(BF16)

    loads[0].wait()
    sending = dot(picking, go_v[...], 1, 0).astype(BF16)
    for h in range(n_exp):
        a_send[h] = sending[h * part : (h + 1) * part]
    pl.semaphore_wait(barrier, n_exp - 1 + n_dp - 1)
    def a_copy(k, src, slot, to):
        return pltpu.make_async_remote_copy(
            src_ref=src,
            dst_ref=a_buf.at[slot],
            send_sem=a_ssem.at[k - 1],
            recv_sem=a_rsem.at[k - 1],
            device_id={"expert": to},
            device_id_type=MESH,
        )

    a_copies = {}
    for k in range(1, n_exp):
        a_copies[k] = a_copy(k, a_send.at[member_at(k)], member, member_at(k))
        a_copies[k].start()
    a_buf[member] = a_send[member]

    loads[1].wait()
    ri = lax.broadcasted_iota(jnp.int32, (rows, rows), 0)
    rj = lax.broadcasted_iota(jnp.int32, (rows, rows), 1)
    wanted = (
        lax.rem(lax.div(ri, CAPS), micro) * (n_exp * CAPS)
        + lax.div(ri, part) * CAPS
        + lax.rem(ri, CAPS)
    )
    inputs = dot(jnp.where(rj == wanted, 1.0, 0.0).astype(BF16), x_v[...], 1, 0).astype(BF16)
    loads[2].wait()
    gate = dot(inputs, wg_v[...], 1, 0)
    loads[3].wait()
    up = dot(inputs, wu_v[...], 1, 0)
    sigmoid = jax.nn.sigmoid(gate)
    activated = gate * sigmoid
    hidden = (activated * up).astype(BF16)
    h_copies, s_copies = [], []
    if gather:
        h_all[replica] = hidden
        for k in range(n_dp - 1, 0, -1):
            copy = pltpu.make_async_remote_copy(
                src_ref=h_all.at[replica],
                dst_ref=h_all.at[replica],
                send_sem=h_ssem.at[k - 1],
                recv_sem=h_rsem.at[k - 1],
                device_id={"dp": flipped(replica, k)},
                device_id_type=MESH,
            )
            copy.start()
            h_copies.append(copy)
    slope = up * sigmoid * (1.0 + gate * (1.0 - sigmoid))
    loads[4].wait()

    def p1_copy(o):
        return pltpu.make_async_remote_copy(
            src_ref=p1_send.at[o, 1 - core],
            dst_ref=p1_buf.at[o],
            send_sem=p1_ssem.at[o],
            recv_sem=p1_rsem.at[o],
            device_id=partner,
            device_id_type=MESH,
        )

    def store_terms(o, value):
        for d in range(n_dp):
            block = value[d * row_block : (d + 1) * row_block]
            acc[o, d % 2, d // 2] = block
            p1_send[o, d % 2, d // 2] = block.astype(BF16)

    p1_copies, p2_copies = {}, {}

    def start_p1(o, value):
        store_terms(o, value)
        p1_copies[o] = p1_copy(o)
        p1_copies[o].start()

    def start_p2(o):
        p1_copies[o].wait_recv()
        for k in range(chips - 1, 0, -1):
            q = flipped(chip, k)
            p2_send[o, q] = (acc[o, core, q] + p1_buf[o, q].astype(F32)).astype(BF16)
            copy = pltpu.make_async_remote_copy(
                src_ref=p2_send.at[o, q],
                dst_ref=p2_buf.at[o, k - 1],
                send_sem=p2_ssem.at[o, k - 1],
                recv_sem=p2_rsem.at[o, k - 1],
                device_id=chip_at(k),
                device_id_type=MESH,
            )
            copy.start()
            p2_copies[o, k] = copy

    for k in range(1, n_exp):
        a_copies[k].wait_recv()
    scaled = a_buf[...].reshape(rows, width)
    if gather:
        for k in range(n_dp - 1, 0, -1):
            peer = flipped(replica, k)
            columns = pl.ds(pl.multiple_of(peer * row_block, row_block), row_block)
            copy = pltpu.make_async_remote_copy(
                src_ref=a_buf.at[:, :, columns],
                dst_ref=s_all.at[replica],
                send_sem=s_ssem.at[k - 1],
                recv_sem=s_rsem.at[k - 1],
                device_id={"dp": peer},
                device_id_type=MESH,
            )
            copy.start()
            s_copies.append(copy)
    else:
        start_p1(0, dot(scaled, hidden, 0, 0))
    dhidden = dot(scaled, wd_v[...], 1, 1)
    d_gate = (dhidden * slope).astype(BF16)
    d_up = (dhidden * activated).astype(BF16)
    returning = (dot(d_gate, wg_v[...], 1, 1) + dot(d_up, wu_v[...], 1, 1)).astype(BF16)
    for h in range(n_exp):
        r_send[h] = returning[h * part : (h + 1) * part]
    r_copies = []
    for k in range(n_exp - 1, 0, -1):
        copy = pltpu.make_async_remote_copy(
            src_ref=r_send.at[member_at(k)],
            dst_ref=r_buf.at[member],
            send_sem=r_ssem.at[k - 1],
            recv_sem=r_rsem.at[k - 1],
            device_id={"expert": member_at(k)},
            device_id_type=MESH,
        )
        copy.start()
        r_copies.append(copy)
    start_p1(1, dot(inputs, d_gate, 0, 0))
    start_p1(2, dot(inputs, d_up, 0, 0))
    if not gather:
        start_p2(0)
    r_buf[member] = r_send[member]
    start_p2(1)
    start_p2(2)

    if gather:
        own = pl.ds(pl.multiple_of(replica * row_block, row_block), row_block)
        s_all[replica] = a_buf[:, :, own]
        for copy in h_copies + s_copies:
            copy.wait_recv()
        slots = n_dp * rows
        down = dot(
            s_all[...].reshape(slots, row_block), h_all[...].reshape(slots, wg_v.shape[1]), 0, 0
        )
        gd_ref[...] = down * (1.0 / (micro * n_dp))
    for copy in r_copies:
        copy.wait_recv()
    gin_ref[...] = dot(mixing, r_buf[...].reshape(rows, width), 0, 0).astype(BF16)

    factor = 1.0 / (micro * n_dp)
    for o, out in enumerate((gd_ref, gg_ref, gu_ref)):
        if o not in p1_copies:
            continue
        total = acc[o, core, chip] + p1_buf[o, chip].astype(F32)
        for k in range(chips - 1, 0, -1):
            p2_copies[o, k].wait_recv()
            total = total + p2_buf[o, k - 1].astype(F32)
        out[...] = total * factor
    started = [*a_copies.values(), *p1_copies.values(), *p2_copies.values()]
    for copy in started + r_copies + h_copies + s_copies:
        copy.wait_send()


def settle(*refs):
    count = len(refs) // 2
    sem = refs[-1]
    copies = [
        pltpu.make_async_copy(refs[i], refs[count + i], sem.at[i]) for i in range(count)
    ]
    for copy in copies:
        copy.start()
    for copy in copies:
        copy.wait()


def settled(arrays):
    anywhere = pl.BlockSpec(memory_space=pl.ANY)
    return pl.pallas_call(
        settle,
        out_shape=tuple(jax.ShapeDtypeStruct(a.shape, a.dtype) for a in arrays),
        in_specs=[pl.BlockSpec(memory_space=pltpu.VMEM)] * len(arrays),
        out_specs=(anywhere,) * len(arrays),
        scratch_shapes=[pltpu.SemaphoreType.DMA((len(arrays),))],
    )(*[pltpu.with_memory_space_constraint(a, pltpu.VMEM) for a in arrays])


def per_device(n_exp, n_dp, grad_out, routes, route_probs, dispatched, w_gate, w_up, w_down):
    micro, tok_dev, width = grad_out.shape
    cols = w_gate.shape[1]
    tokens = micro * tok_dev
    part = micro * CAPS
    rows = n_exp * part
    chips = n_dp // 2
    row_block = width // n_dp
    vmem = pl.BlockSpec(memory_space=pltpu.VMEM)
    hbm = pl.BlockSpec(memory_space=pl.ANY)
    grad = pltpu.VMEM((row_block, cols), F32)
    dma = pltpu.SemaphoreType.DMA
    others = max(chips - 1, 1)
    gather = row_block % 128 == 0
    out = pl.pallas_call(
        functools.partial(kernel, micro, n_exp, n_dp),
        out_shape=(pltpu.VMEM((tokens, width), BF16), grad, grad, grad),
        in_specs=[vmem, vmem, hbm, hbm, hbm, hbm, hbm],
        out_specs=(vmem, vmem, vmem, vmem),
        scratch_shapes=[
            pltpu.VMEM((tokens, width), BF16),
            pltpu.VMEM((rows, width), BF16),
            pltpu.VMEM((width, cols), BF16),
            pltpu.VMEM((width, cols), BF16),
            pltpu.VMEM((cols, width), BF16),
            pltpu.VMEM((n_exp, part, width), BF16),
            pltpu.VMEM((n_exp, part, width), BF16),
            pltpu.VMEM((n_exp, part, width), BF16),
            pltpu.VMEM((n_exp, part, width), BF16),
            pltpu.VMEM((3, 2, chips, row_block, cols), F32),
            pltpu.VMEM((3, 2, chips, row_block, cols), BF16),
            pltpu.VMEM((3, chips, row_block, cols), BF16),
            pltpu.VMEM((3, chips, row_block, cols), BF16),
            pltpu.VMEM((3, others, row_block, cols), BF16),
            pltpu.VMEM((n_dp, n_exp, part, row_block) if gather else (8, 128), BF16),
            pltpu.VMEM((n_dp, rows, cols) if gather else (8, 128), BF16),
            dma((5,)),
            dma((n_exp - 1,)),
            dma((n_exp - 1,)),
            dma((n_exp - 1,)),
            dma((n_exp - 1,)),
            dma((3,)),
            dma((3,)),
            dma((3, others)),
            dma((3, others)),
            dma((n_dp - 1,)),
            dma((n_dp - 1,)),
            dma((n_dp - 1,)),
            dma((n_dp - 1,)),
        ],
        compiler_params=pltpu.CompilerParams(collective_id=0, has_side_effects=True),
    )(
        routes.transpose(0, 2, 1),
        route_probs.transpose(0, 2, 1),
        grad_out.reshape(tokens, width),
        dispatched.reshape(rows, width),
        w_gate,
        w_up,
        w_down,
    )
    out = settled(out)
    return (out[0].reshape(micro, tok_dev, width),) + tuple(out[1:])


def solution(mesh):
    return jax.shard_map(
        functools.partial(per_device, mesh.shape["expert"], mesh.shape["dp"]),
        mesh=mesh,
        in_specs=(
            P(None, ("dp", "expert"), None),
            P(None, ("dp", "expert"), None),
            P(None, ("dp", "expert"), None),
            P(None, ("dp", "expert"), None),
            P(None, "expert"),
            P(None, "expert"),
            P("expert", None),
        ),
        out_specs=(
            P(None, ("dp", "expert"), None),
            P("dp", "expert"),
            P("dp", "expert"),
            P("dp", "expert"),
        ),
        check_vma=False,
    )
```

profile of v0, /device:TPU:0, one launch (start us, length us, event | category | flops | bytes accessed | tf_op | source)
XLA Modules:
  0.0 25.0 jit_solution(17597871030325692086)
XLA Ops:
  0.6 23.4 %shard_map.102 = (bf16[256,1024]{1,0:T(8,128)(2,1)S(1)}, f32[128,256]{1,0:T(8,128)S(1)}, f32[128,256]{1,0:T(8,128)S(1)}, f32[128,256]{1,0:T(8,128)S(1)}) custom-call(s32[4,8,64]{2,1,0:T(8,128)} %bitcast.7, bf16[4,8,64]{2,1,0:T(8,128)(2,1)} %bitcast.8, bf16[256,1024]{1,0:T(8,128)(2,1)} %bitcast.5, bf16[128,1024]{1,0:T(8,128)(2,1)} %bitcast.6, ...), custom_call_target="tpu_custom_call" | custom-call | tf_op jit(solution)/shard_map/pallas_call | solution.py:347
  24.0 1.0 %shard_map.103 = (bf16[256,1024]{1,0:T(8,128)(2,1)}, f32[128,256]{1,0:T(8,128)}, f32[128,256]{1,0:T(8,128)}, f32[128,256]{1,0:T(8,128)}) custom-call(bf16[256,1024]{1,0:T(8,128)(2,1)S(1)} %get-tuple-element.12.refs_0_, f32[128,256]{1,0:T(8,128)S(1)} %get-tuple-element.13.refs_1_, f32[128,256]{1,0:T(8,128)S(1)} %get-tuple-element.14.refs_2_, ...), custom_call_target="tpu_custom_call" | custom-call | tf_op jit(solution)/shard_map/pallas_call | solution.py:324
where the time goes:
time: 25.3 us; the launch traced here: 25 us
  Pallas kernels  24.3 us (96%)
  between operations  0.64 us (3%)
    pallas_call x1, Pallas kernels, per_device(): pl.pallas_call(functools.partial(kernel, micro, n_exp, n_dp), out_shape=(...  23.4 us
    pallas_call x1, Pallas kernels, settled(): pl.pallas_call(settle, out_shape=tuple((jax.ShapeDtypeStruct(a.shape, a.d...  0.95 us

commit v1 on v0

--- a/solution.py
+++ b/solution.py
@@ -307,6 +307,318 @@
         copy.wait_send()
 
 
+def pooled_kernel(
+    micro,
+    n_exp,
+    n_dp,
+    routes_hbm,
+    probs_hbm,
+    go_hbm,
+    x_hbm,
+    wg_hbm,
+    wu_hbm,
+    wd_hbm,
+    gin_ref,
+    gg_ref,
+    gu_ref,
+    gd_ref,
+    routes_v,
+    probs_v,
+    go_v,
+    x_v,
+    x_par,
+    xt_v,
+    wg_v,
+    wu_v,
+    wd_v,
+    a_send,
+    a_buf,
+    r_send,
+    r_buf,
+    mix_v,
+    d_all,
+    relay_send,
+    relay_buf,
+    last_send,
+    last_buf,
+    s_all,
+    h_all,
+    down_v,
+    down_buf,
+    load_sem,
+    a_ssem,
+    a_rsem,
+    r_ssem,
+    r_rsem,
+    x_sem,
+    d_sem,
+    relay_ssem,
+    relay_rsem,
+    last_ssem,
+    last_rsem,
+    s_ssem,
+    s_rsem,
+    h_ssem,
+    h_rsem,
+    down_sem,
+):
+    member = lax.axis_index("expert")
+    replica = lax.axis_index("dp")
+    core = lax.rem(replica, 2)
+    chip = lax.div(replica, 2)
+    chips = n_dp // 2
+    partner = {"dp": chip * 2 + 1 - core}
+    window = n_exp // 2
+    tokens, width = go_v.shape
+    cols = wg_v.shape[1]
+    tok_dev = tokens // micro
+    part = micro * CAPS
+    rows = n_exp * part
+    row_block = width // n_dp
+    pair_block = 2 * row_block
+    hops = range(chips - 1, 0, -1)
+
+    loads = [
+        pltpu.make_async_copy(src, dst, load_sem.at[i])
+        for i, (src, dst) in enumerate(
+            (
+                (routes_hbm, routes_v),
+                (probs_hbm, probs_v),
+                (go_hbm, go_v),
+                *((x_hbm.at[m], x_v.at[:, pl.ds(m * CAPS, CAPS), :]) for m in range(micro)),
+                (wg_hbm, wg_v),
+                (wu_hbm, wu_v),
+                (wd_hbm, wd_v),
+            )
+        )
+    ]
+    for load in loads:
+        load.start()
+
+    def chip_at(k):
+        return flipped(chip, k)
+
+    def peer_at(k):
+        return {"dp": chip_at(k) * 2 + core}
+
+    barrier = pltpu.get_barrier_semaphore()
+    for k in range(1, n_exp):
+        pl.semaphore_signal(
+            barrier, inc=1, device_id={"expert": flipped(member, k)}, device_id_type=MESH
+        )
+    for k in hops:
+        pl.semaphore_signal(barrier, inc=1, device_id=peer_at(k), device_id_type=MESH)
+    pl.semaphore_signal(barrier, inc=1, device_id=partner, device_id_type=MESH)
+
+    started = []
+
+    def remote(src, dst, send_sem, recv_sem, device):
+        copy = pltpu.make_async_remote_copy(
+            src_ref=src,
+            dst_ref=dst,
+            send_sem=send_sem,
+            recv_sem=recv_sem,
+            device_id=device,
+            device_id_type=MESH,
+        )
+        copy.start()
+        started.append(copy)
+        return copy
+
+    pad = max(window, 8)
+    expert_row = lax.broadcasted_iota(jnp.int32, (pad, tokens), 0)
+    ti = lax.broadcasted_iota(jnp.int32, (tokens, tokens), 0)
+    tj = lax.broadcasted_iota(jnp.int32, (tokens, tokens), 1)
+    earlier = jnp.where((ti < tj) & (lax.div(ti, tok_dev) == lax.div(tj, tok_dev)), 1.0, 0.0)
+    loads[0].wait()
+    loads[1].wait()
+    ids = jnp.concatenate([routes_v[m] for m in range(micro)], axis=1)
+    probs = jnp.concatenate([probs_v[m].astype(F32) for m in range(micro)], axis=1)
+    hits, weights = [], []
+    table = jnp.zeros((pad, tokens), F32)
+    for e in range(window):
+        named = ids == e
+        hits.append(jnp.sum(jnp.where(named, 1.0, 0.0), axis=0, keepdims=True))
+        weights.append(jnp.sum(jnp.where(named, probs, 0.0), axis=0, keepdims=True))
+        table = jnp.where(expert_row == e, hits[e], table)
+    ranking = dot(table.astype(BF16), earlier.astype(BF16), 1, 0)
+    slot = lax.broadcasted_iota(jnp.int32, (CAPS, tokens), 0).astype(F32)
+    batch = lax.div(lax.broadcasted_iota(jnp.int32, (CAPS, tokens), 1), tok_dev)
+    ones, scales = [], []
+    for e in range(window):
+        chosen = (hits[e] > 0.5) & (ranking[e : e + 1] == slot)
+        for m in range(micro):
+            here = chosen & (batch == m)
+            ones.append(jnp.where(here, 1.0, 0.0))
+            scales.append(jnp.where(here, weights[e], 0.0))
+    picking = jnp.concatenate(scales, axis=0).astype(BF16)
+
+    loads[2].wait()
+    sending = dot(picking, go_v[...], 1, 0).astype(BF16)
+    for e in range(window):
+        a_send[e] = sending[e * part : (e + 1) * part]
+    pl.semaphore_wait(barrier, n_exp - 1 + chips)
+
+    order = [flipped(member, k) for k in range(n_exp - 1, 0, -1)]
+    nearest = order[::-1]
+    for j, to in enumerate(order):
+        remote(
+            a_send.at[lax.div(to, 2)],
+            a_buf.at[member],
+            a_ssem.at[j],
+            a_rsem.at[member],
+            {"expert": to},
+        )
+    a_buf[member] = a_send[lax.div(member, 2)]
+
+    def a_arrival(source):
+        return pltpu.make_async_remote_copy(
+            src_ref=a_send.at[0],
+            dst_ref=a_buf.at[source],
+            send_sem=a_ssem.at[0],
+            recv_sem=a_rsem.at[source],
+            device_id={"expert": source},
+            device_id_type=MESH,
+        )
+
+    for m in range(micro):
+        loads[3 + m].wait()
+    x_copy = remote(x_v, x_par, x_sem.at[0], x_sem.at[1], partner)
+
+    inputs = x_v[...].reshape(rows, width)
+    loads[3 + micro].wait()
+    gate = dot(inputs, wg_v[...], 1, 0)
+    loads[4 + micro].wait()
+    up = dot(inputs, wu_v[...], 1, 0)
+    sigmoid = jax.nn.sigmoid(gate)
+    activated = gate * sigmoid
+    h_all[chip] = (activated * up).astype(BF16)
+    h_copies = {
+        k: remote(
+            h_all.at[chip], h_all.at[chip], h_ssem.at[k - 1], h_rsem.at[k - 1], peer_at(k)
+        )
+        for k in hops
+    }
+    slope = up * sigmoid * (1.0 + gate * (1.0 - sigmoid))
+
+    def blocks(q):
+        return pl.ds(pl.multiple_of(q * pair_block, pair_block), pair_block)
+
+    def send_slices(source, j):
+        for k in hops:
+            remote(
+                a_buf.at[source, :, blocks(chip_at(k))],
+                s_all.at[chip, source],
+                s_ssem.at[j, k - 1],
+                s_rsem.at[k - 1],
+                peer_at(k),
+            )
+
+    send_slices(member, 0)
+
+    mix_v[...] = jnp.concatenate(
+        [jnp.concatenate(ones[e * micro : (e + 1) * micro], axis=0) for e in range(window) for _ in range(2)],
+        axis=0,
+    ).astype(BF16)
+    loads[5 + micro].wait()
+    x_copy.wait_recv()
+    for k in range(chips):
+        q = chip_at(k) if k else chip
+        own = pl.ds(pl.multiple_of((q * 2 + core) * row_block, row_block), row_block)
+        mine = x_v[:, :, own].reshape(rows, row_block)
+        other = x_par[:, :, own].reshape(rows, row_block)
+        xt_v[k] = jnp.concatenate([mine, other], axis=0).T
+
+    for j, source in enumerate(nearest):
+        a_arrival(source).wait_recv()
+        if j < n_exp - 2:
+            send_slices(source, j + 1)
+    scaled = a_buf[...].reshape(rows, width)
+    dhidden = dot(scaled, wd_v[...], 1, 1)
+    d_gate = (dhidden * slope).astype(BF16)
+    d_up = (dhidden * activated).astype(BF16)
+    d_all[0, :, :cols] = d_gate
+    d_all[0, :, cols:] = d_up
+    d_copy = remote(d_all.at[0], d_all.at[1], d_sem.at[0], d_sem.at[1], partner)
+    send_slices(nearest[-1], n_exp - 1)
+
+    returning = (dot(d_gate, wg_v[...], 1, 1) + dot(d_up, wu_v[...], 1, 1)).astype(BF16)
+    for h in range(n_exp):
+        r_send[h] = returning[h * part : (h + 1) * part]
+    r_copies = [
+        remote(
+            r_send.at[to], r_buf.at[member], r_ssem.at[k - 1], r_rsem.at[k - 1], {"expert": to}
+        )
+        for k, to in zip(range(n_exp - 1, 0, -1), order)
+    ]
+
+    d_copy.wait_recv()
+    factors = d_all[...].reshape(2 * rows, 2 * cols)
+    far = dot(xt_v[3], factors, 1, 0).astype(BF16)
+    relays = []
+    for i, k in enumerate((1, 2)):
+        relay_send[i] = far[:, i * cols : (i + 1) * cols]
+        relays.append(
+            remote(
+                relay_send.at[i],
+                relay_buf.at[i],
+                relay_ssem.at[i],
+                relay_rsem.at[i],
+                peer_at(k),
+            )
+        )
+
+    def send_last(i, k, value):
+        last_send[i] = value.astype(BF16)
+        return remote(
+            last_send.at[i], last_buf.at[i], last_ssem.at[i], last_rsem.at[i], peer_at(k)
+        )
+
+    near = [dot(xt_v[k], factors, 1, 0) for k in (1, 2)]
+    last_copies = [
+        send_last(0, 1, near[0][:, :cols]),
+        send_last(1, 2, near[1][:, cols:]),
+    ]
+    total = dot(xt_v[0], factors, 1, 0)
+    r_buf[member] = r_send[member]
+    s_all[chip] = a_buf[:, :, blocks(chip)]
+    relays[0].wait_recv()
+    last_copies.append(send_last(2, 2, near[1][:, :cols] + relay_buf[0].astype(F32)))
+    relays[1].wait_recv()
+    last_copies.append(send_last(3, 1, near[0][:, cols:] + relay_buf[1].astype(F32)))
+    for k in hops:
+        h_copies[k].wait_recv()
+        pltpu.make_async_remote_copy(
+            src_ref=s_all.at[chip],
+            dst_ref=s_all.at[chip_at(k)],
+            send_sem=s_ssem.at[0, k - 1],
+            recv_sem=s_rsem.at[k - 1],
+            device_id=peer_at(k),
+            device_id_type=MESH,
+        ).wait_recv()
+    slots = chips * rows
+    down = dot(s_all[...].reshape(slots, pair_block), h_all[...].reshape(slots, cols), 0, 0)
+    down_v[0] = down[:row_block]
+    down_v[1] = down[row_block:]
+    down_copy = remote(down_v.at[1 - core], down_buf, down_sem.at[0], down_sem.at[1], partner)
+
+    for copy in r_copies:
+        copy.wait_recv()
+    gin_ref[...] = dot(mix_v[...], r_buf[...].reshape(rows, width), 0, 0).astype(BF16)
+
+    factor = 1.0 / (micro * n_dp)
+    down_copy.wait_recv()
+    gd_ref[...] = (down_v[core] + down_buf[...]) * factor
+    for copy in last_copies:
+        copy.wait_recv()
+    gates = total[:, :cols] + last_buf[0].astype(F32) + last_buf[2].astype(F32)
+    ups = total[:, cols:] + last_buf[1].astype(F32) + last_buf[3].astype(F32)
+    gg_ref[...] = gates * factor
+    gu_ref[...] = ups * factor
+    for copy in started:
+        copy.wait_send()
+
+
 def settle(*refs):
     count = len(refs) // 2
     sem = refs[-1]
@@ -330,7 +642,77 @@
     )(*[pltpu.with_memory_space_constraint(a, pltpu.VMEM) for a in arrays])
 
 
-def per_device(n_exp, n_dp, grad_out, routes, route_probs, dispatched, w_gate, w_up, w_down):
+def pooled_call(n_exp, n_dp, grad_out, routes, route_probs, dispatched, w_gate, w_up, w_down):
+    micro, tok_dev, width = grad_out.shape
+    cols = w_gate.shape[1]
+    tokens = micro * tok_dev
+    part = micro * CAPS
+    rows = n_exp * part
+    chips = n_dp // 2
+    row_block = width // n_dp
+    vmem = pl.BlockSpec(memory_space=pltpu.VMEM)
+    hbm = pl.BlockSpec(memory_space=pl.ANY)
+    grad = pltpu.VMEM((row_block, cols), F32)
+    dma = pltpu.SemaphoreType.DMA
+    return pl.pallas_call(
+        functools.partial(pooled_kernel, micro, n_exp, n_dp),
+        out_shape=(pltpu.VMEM((tokens, width), BF16), grad, grad, grad),
+        in_specs=[hbm] * 7,
+        out_specs=(vmem, vmem, vmem, vmem),
+        scratch_shapes=[
+            pltpu.VMEM((micro, routes.shape[2], tok_dev), jnp.int32),
+            pltpu.VMEM((micro, routes.shape[2], tok_dev), BF16),
+            pltpu.VMEM((tokens, width), BF16),
+            pltpu.VMEM((n_exp, part, width), BF16),
+            pltpu.VMEM((n_exp, part, width), BF16),
+            pltpu.VMEM((chips, row_block, 2 * rows), BF16),
+            pltpu.VMEM((width, cols), BF16),
+            pltpu.VMEM((width, cols), BF16),
+            pltpu.VMEM((cols, width), BF16),
+            pltpu.VMEM((n_exp // 2, part, width), BF16),
+            pltpu.VMEM((n_exp, part, width), BF16),
+            pltpu.VMEM((n_exp, part, width), BF16),
+            pltpu.VMEM((n_exp, part, width), BF16),
+            pltpu.VMEM((rows, tokens), BF16),
+            pltpu.VMEM((2, rows, 2 * cols), BF16),
+            pltpu.VMEM((2, row_block, cols), BF16),
+            pltpu.VMEM((2, row_block, cols), BF16),
+            pltpu.VMEM((4, row_block, cols), BF16),
+            pltpu.VMEM((4, row_block, cols), BF16),
+            pltpu.VMEM((chips, n_exp, part, 2 * row_block), BF16),
+            pltpu.VMEM((chips, rows, cols), BF16),
+            pltpu.VMEM((2, row_block, cols), F32),
+            pltpu.VMEM((row_block, cols), F32),
+            dma((6 + micro,)),
+            dma((n_exp - 1,)),
+            dma((n_exp,)),
+            dma((n_exp - 1,)),
+            dma((n_exp - 1,)),
+            dma((2,)),
+            dma((2,)),
+            dma((2,)),
+            dma((2,)),
+            dma((4,)),
+            dma((4,)),
+            dma((n_exp, chips - 1)),
+            dma((chips - 1,)),
+            dma((chips - 1,)),
+            dma((chips - 1,)),
+            dma((2,)),
+        ],
+        compiler_params=pltpu.CompilerParams(collective_id=0, has_side_effects=True),
+    )(
+        routes.transpose(0, 2, 1),
+        route_probs.transpose(0, 2, 1),
+        grad_out.reshape(tokens, width),
+        dispatched.reshape(micro, n_exp, CAPS, width),
+        w_gate,
+        w_up,
+        w_down,
+    )
+
+
+def spread_call(n_exp, n_dp, grad_out, routes, route_probs, dispatched, w_gate, w_up, w_down):
     micro, tok_dev, width = grad_out.shape
     cols = w_gate.shape[1]
     tokens = micro * tok_dev
@@ -344,7 +726,7 @@
     dma = pltpu.SemaphoreType.DMA
     others = max(chips - 1, 1)
     gather = row_block % 128 == 0
-    out = pl.pallas_call(
+    return pl.pallas_call(
         functools.partial(kernel, micro, n_exp, n_dp),
         out_shape=(pltpu.VMEM((tokens, width), BF16), grad, grad, grad),
         in_specs=[vmem, vmem, hbm, hbm, hbm, hbm, hbm],
@@ -390,8 +772,13 @@
         w_up,
         w_down,
     )
-    out = settled(out)
-    return (out[0].reshape(micro, tok_dev, width),) + tuple(out[1:])
+
+
+def per_device(n_exp, n_dp, grad_out, *rest):
+    pooled = n_exp == 4 and n_dp == 8 and (grad_out.shape[2] // n_dp) % 128 == 0
+    call = pooled_call if pooled else spread_call
+    out = settled(call(n_exp, n_dp, grad_out, *rest))
+    return (out[0].reshape(grad_out.shape),) + tuple(out[1:])
 
 
 def solution(mesh):

time: 25.3 us -> 23.8 us (0.941)
  Pallas kernels: 24.3 us -> 22.9 us
    pallas_call x1, Pallas kernels: 23.4 us -> 21.9 us  [pooled_call(): pl.pallas_call(functools.partial(pooled_kernel, micro, n_exp, n_dp), out_...]
where the time goes in v1:
time: 23.8 us; the launch traced here: 23.5 us
  Pallas kernels  22.9 us (96%)
  between operations  0.64 us (3%)
    pallas_call x1, Pallas kernels, pooled_call(): pl.pallas_call(functools.partial(pooled_kernel, micro, n_exp, n_dp), out_...  21.9 us
    pallas_call x1, Pallas kernels, settled(): pl.pallas_call(settle, out_shape=tuple((jax.ShapeDtypeStruct(a.shape, a.d...  0.95 us

profile of v1, /device:TPU:0, one launch (start us, length us, event | category | flops | bytes accessed | tf_op | source)
XLA Modules:
  0.0 23.5 jit_solution(16730385694977068737)
XLA Ops:
  0.6 21.9 %shard_map.102 = (bf16[256,1024]{1,0:T(8,128)(2,1)S(1)}, f32[128,256]{1,0:T(8,128)S(1)}, f32[128,256]{1,0:T(8,128)S(1)}, f32[128,256]{1,0:T(8,128)S(1)}) custom-call(s32[4,8,64]{2,1,0:T(8,128)} %bitcast.7, bf16[4,8,64]{2,1,0:T(8,128)(2,1)} %bitcast.8, bf16[256,1024]{1,0:T(8,128)(2,1)} %bitcast.5, bf16[4,4,8,1024]{3,2,1,0:T(8,128)(2,1)} %bitcast.6, ...), custom_call_target="tpu_custom_call" | custom-call | tf_op jit(solution)/shard_map/pallas_call | solution.py:657
  22.6 1.0 %shard_map.103 = (bf16[256,1024]{1,0:T(8,128)(2,1)}, f32[128,256]{1,0:T(8,128)}, f32[128,256]{1,0:T(8,128)}, f32[128,256]{1,0:T(8,128)}) custom-call(bf16[256,1024]{1,0:T(8,128)(2,1)S(1)} %get-tuple-element.12.refs_0_, f32[128,256]{1,0:T(8,128)S(1)} %get-tuple-element.13.refs_1_, f32[128,256]{1,0:T(8,128)S(1)} %get-tuple-element.14.refs_2_, ...), custom_call_target="tpu_custom_call" | custom-call | tf_op jit(solution)/shard_map/pallas_call | solution.py:636

commit v2 on v1

--- a/solution.py
+++ b/solution.py
@@ -459,8 +459,13 @@
         a_send[e] = sending[e * part : (e + 1) * part]
     pl.semaphore_wait(barrier, n_exp - 1 + chips)
 
-    order = [flipped(member, k) for k in range(n_exp - 1, 0, -1)]
-    nearest = order[::-1]
+    inner = jnp.where((member == 0) | (member == n_exp - 1), 0, 1)
+    order = [
+        flipped(member, 1) * (1 - inner) + flipped(member, 2) * inner,
+        flipped(member, 3),
+        flipped(member, 2) * (1 - inner) + flipped(member, 1) * inner,
+    ]
+    nearest = [flipped(member, 1), flipped(member, 3) * inner + flipped(member, 2) * (1 - inner), flipped(member, 2) * inner + flipped(member, 3) * (1 - inner)]
     for j, to in enumerate(order):
         remote(
             a_send.at[lax.div(to, 2)],
@@ -542,15 +547,44 @@
     d_copy = remote(d_all.at[0], d_all.at[1], d_sem.at[0], d_sem.at[1], partner)
     send_slices(nearest[-1], n_exp - 1)
 
-    returning = (dot(d_gate, wg_v[...], 1, 1) + dot(d_up, wu_v[...], 1, 1)).astype(BF16)
-    for h in range(n_exp):
-        r_send[h] = returning[h * part : (h + 1) * part]
+    pieces = 1
+    piece = width // pieces
+
+    def span(c):
+        return pl.ds(c * piece, piece)
+
     r_copies = [
-        remote(
-            r_send.at[to], r_buf.at[member], r_ssem.at[k - 1], r_rsem.at[k - 1], {"expert": to}
-        )
-        for k, to in zip(range(n_exp - 1, 0, -1), order)
+        [
+            pltpu.make_async_remote_copy(
+                src_ref=r_send.at[to, :, span(c)],
+                dst_ref=r_buf.at[member, :, span(c)],
+                send_sem=r_ssem.at[c, j],
+                recv_sem=r_rsem.at[c, member],
+                device_id={"expert": to},
+                device_id_type=MESH,
+            )
+            for j, to in enumerate(order)
+        ]
+        for c in range(pieces)
     ]
+    started.extend(copy for copies in r_copies for copy in copies)
+
+    def send_back():
+        for c in range(pieces):
+            returning = dot(d_all[0, :, :cols], wg_v[span(c), :], 1, 1) + dot(
+                d_all[0, :, cols:], wu_v[span(c), :], 1, 1
+            )
+            returning = returning.astype(BF16)
+            for h in range(n_exp):
+                r_send[h, :, span(c)] = returning[h * part : (h + 1) * part]
+            for copy in r_copies[c]:
+                copy.start()
+
+    returns_first = core == 1
+
+    @pl.when(returns_first)
+    def _():
+        send_back()
 
     d_copy.wait_recv()
     factors = d_all[...].reshape(2 * rows, 2 * cols)
@@ -580,6 +614,10 @@
         send_last(1, 2, near[1][:, cols:]),
     ]
     total = dot(xt_v[0], factors, 1, 0)
+    @pl.when(jnp.logical_not(returns_first))
+    def _():
+        send_back()
+
     r_buf[member] = r_send[member]
     s_all[chip] = a_buf[:, :, blocks(chip)]
     relays[0].wait_recv()
@@ -602,9 +640,19 @@
     down_v[1] = down[row_block:]
     down_copy = remote(down_v.at[1 - core], down_buf, down_sem.at[0], down_sem.at[1], partner)
 
-    for copy in r_copies:
-        copy.wait_recv()
-    gin_ref[...] = dot(mix_v[...], r_buf[...].reshape(rows, width), 0, 0).astype(BF16)
+    for c in range(pieces):
+        for source in order:
+            pltpu.make_async_remote_copy(
+                src_ref=r_send.at[source, :, span(c)],
+                dst_ref=r_buf.at[source, :, span(c)],
+                send_sem=r_ssem.at[c, 0],
+                recv_sem=r_rsem.at[c, source],
+                device_id={"expert": source},
+                device_id_type=MESH,
+            ).wait_recv()
+        gin_ref[:, span(c)] = dot(
+            mix_v[...], r_buf[:, :, span(c)].reshape(rows, piece), 0, 0
+        ).astype(BF16)
 
     factor = 1.0 / (micro * n_dp)
     down_copy.wait_recv()
@@ -686,8 +734,8 @@
             dma((6 + micro,)),
             dma((n_exp - 1,)),
             dma((n_exp,)),
-            dma((n_exp - 1,)),
-            dma((n_exp - 1,)),
+            dma((1, n_exp - 1)),
+            dma((1, n_exp)),
             dma((2,)),
             dma((2,)),
             dma((2,)),

time: 23.8 us -> 21.8 us (0.916)
  Pallas kernels: 22.9 us -> 20.9 us
    pallas_call x1, Pallas kernels: 21.9 us -> 20 us  [pooled_call(): pl.pallas_call(functools.partial(pooled_kernel, micro, n_exp, n_dp), out_...]
where the time goes in v2:
time: 21.8 us; the launch traced here: 21.6 us
  Pallas kernels  20.9 us (96%)
  between operations  0.64 us (3%)
    pallas_call x1, Pallas kernels, pooled_call(): pl.pallas_call(functools.partial(pooled_kernel, micro, n_exp, n_dp), out_...  20 us
    pallas_call x1, Pallas kernels, settled(): pl.pallas_call(settle, out_shape=tuple((jax.ShapeDtypeStruct(a.shape, a.d...  0.95 us

profile of v2, /device:TPU:0, one launch (start us, length us, event | category | flops | bytes accessed | tf_op | source)
XLA Modules:
  0.0 21.6 jit_solution(11403598510179693864)
XLA Ops:
  0.6 20.0 %shard_map.102 = (bf16[256,1024]{1,0:T(8,128)(2,1)S(1)}, f32[128,256]{1,0:T(8,128)S(1)}, f32[128,256]{1,0:T(8,128)S(1)}, f32[128,256]{1,0:T(8,128)S(1)}) custom-call(s32[4,8,64]{2,1,0:T(8,128)} %bitcast.7, bf16[4,8,64]{2,1,0:T(8,128)(2,1)} %bitcast.8, bf16[256,1024]{1,0:T(8,128)(2,1)} %bitcast.5, bf16[4,4,8,1024]{3,2,1,0:T(8,128)(2,1)} %bitcast.6, ...), custom_call_target="tpu_custom_call" | custom-call | tf_op jit(solution)/shard_map/pallas_call | solution.py:705
  20.6 1.0 %shard_map.103 = (bf16[256,1024]{1,0:T(8,128)(2,1)}, f32[128,256]{1,0:T(8,128)}, f32[128,256]{1,0:T(8,128)}, f32[128,256]{1,0:T(8,128)}) custom-call(bf16[256,1024]{1,0:T(8,128)(2,1)S(1)} %get-tuple-element.12.refs_0_, f32[128,256]{1,0:T(8,128)S(1)} %get-tuple-element.13.refs_1_, f32[128,256]{1,0:T(8,128)S(1)} %get-tuple-element.14.refs_2_, ...), custom_call_target="tpu_custom_call" | custom-call | tf_op jit(solution)/shard_map/pallas_call | solution.py:684

commit v3 on v1

--- a/solution.py
+++ b/solution.py
@@ -337,7 +337,6 @@
     r_buf,
     mix_v,
     d_all,
-    relay_send,
     relay_buf,
     last_send,
     last_buf,
@@ -345,21 +344,16 @@
     h_all,
     down_v,
     down_buf,
+    sized,
     load_sem,
-    a_ssem,
-    a_rsem,
-    r_ssem,
-    r_rsem,
+    sent_sem,
+    a_sem,
+    r_sem,
     x_sem,
     d_sem,
-    relay_ssem,
-    relay_rsem,
-    last_ssem,
-    last_rsem,
-    s_ssem,
-    s_rsem,
-    h_ssem,
-    h_rsem,
+    relay_sem,
+    last_sem,
+    slot_sem,
     down_sem,
 ):
     member = lax.axis_index("expert")
@@ -378,8 +372,23 @@
     pair_block = 2 * row_block
     hops = range(chips - 1, 0, -1)
 
+    def chip_at(k):
+        return flipped(chip, k)
+
+    def peer_at(k):
+        return {"dp": chip_at(k) * 2 + core}
+
+    barrier = pltpu.get_barrier_semaphore()
+    for k in range(n_exp - 1, 0, -1):
+        pl.semaphore_signal(
+            barrier, inc=1, device_id={"expert": flipped(member, k)}, device_id_type=MESH
+        )
+    for k in hops:
+        pl.semaphore_signal(barrier, inc=1, device_id=peer_at(k), device_id_type=MESH)
+    pl.semaphore_signal(barrier, inc=1, device_id=partner, device_id_type=MESH)
+
     loads = [
-        pltpu.make_async_copy(src, dst, load_sem.at[i])
+        pltpu.make_async_copy(src, dst, load_sem.at[min(i, 3)])
         for i, (src, dst) in enumerate(
             (
                 (routes_hbm, routes_v),
@@ -395,34 +404,26 @@
     for load in loads:
         load.start()
 
-    def chip_at(k):
-        return flipped(chip, k)
-
-    def peer_at(k):
-        return {"dp": chip_at(k) * 2 + core}
-
-    barrier = pltpu.get_barrier_semaphore()
-    for k in range(1, n_exp):
-        pl.semaphore_signal(
-            barrier, inc=1, device_id={"expert": flipped(member, k)}, device_id_type=MESH
-        )
-    for k in hops:
-        pl.semaphore_signal(barrier, inc=1, device_id=peer_at(k), device_id_type=MESH)
-    pl.semaphore_signal(barrier, inc=1, device_id=partner, device_id_type=MESH)
-
-    started = []
-
-    def remote(src, dst, send_sem, recv_sem, device):
+    def arrivals(size, sem):
+        return pltpu.make_async_copy(sized.at[pl.ds(0, size)], sized.at[pl.ds(0, size)], sem)
+
+    sent = []
+
+    def remote(src, dst, sem, device, start=True):
         copy = pltpu.make_async_remote_copy(
             src_ref=src,
             dst_ref=dst,
-            send_sem=send_sem,
-            recv_sem=recv_sem,
+            send_sem=sent_sem.at[0],
+            recv_sem=sem,
             device_id=device,
             device_id_type=MESH,
         )
-        copy.start()
-        started.append(copy)
+        if start:
+            copy.start()
+            bulk = 1
+            for n in src.shape:
+                bulk *= n
+            sent.append(bulk * (2 if src.dtype == F32 else 1))
         return copy
 
     pad = max(window, 8)
@@ -459,69 +460,57 @@
         a_send[e] = sending[e * part : (e + 1) * part]
     pl.semaphore_wait(barrier, n_exp - 1 + chips)
 
-    order = [flipped(member, k) for k in range(n_exp - 1, 0, -1)]
-    nearest = order[::-1]
-    for j, to in enumerate(order):
-        remote(
-            a_send.at[lax.div(to, 2)],
-            a_buf.at[member],
-            a_ssem.at[j],
-            a_rsem.at[member],
-            {"expert": to},
-        )
+    inner = jnp.where((member == 0) | (member == n_exp - 1), 0, 1)
+    order = [1 + inner, 3, 2 - inner]
+    arriving = [1, 2 + inner, 3 - inner]
+
+    def member_at(k):
+        low, high = lax.rem(k, 2), lax.div(k, 2)
+        low = low * (1 - 2 * lax.rem(member, 2))
+        high = high * (2 - 4 * lax.div(member, 2))
+        return member + low + high
+
+    for k in order:
+        to = member_at(k)
+        remote(a_send.at[lax.div(to, 2)], a_buf.at[member], a_sem.at[k - 1], {"expert": to})
     a_buf[member] = a_send[lax.div(member, 2)]
 
-    def a_arrival(source):
-        return pltpu.make_async_remote_copy(
-            src_ref=a_send.at[0],
-            dst_ref=a_buf.at[source],
-            send_sem=a_ssem.at[0],
-            recv_sem=a_rsem.at[source],
-            device_id={"expert": source},
-            device_id_type=MESH,
-        )
-
-    for m in range(micro):
-        loads[3 + m].wait()
-    x_copy = remote(x_v, x_par, x_sem.at[0], x_sem.at[1], partner)
-
+    weights_rows = width * cols // width
+    arrivals(rows + 3 * weights_rows, load_sem.at[3]).wait()
+    remote(x_v, x_par, x_sem.at[0], partner)
     inputs = x_v[...].reshape(rows, width)
-    loads[3 + micro].wait()
     gate = dot(inputs, wg_v[...], 1, 0)
-    loads[4 + micro].wait()
     up = dot(inputs, wu_v[...], 1, 0)
     sigmoid = jax.nn.sigmoid(gate)
     activated = gate * sigmoid
     h_all[chip] = (activated * up).astype(BF16)
-    h_copies = {
-        k: remote(
-            h_all.at[chip], h_all.at[chip], h_ssem.at[k - 1], h_rsem.at[k - 1], peer_at(k)
-        )
-        for k in hops
-    }
+    for k in hops:
+        remote(h_all.at[chip], h_all.at[chip], slot_sem.at[0], peer_at(k))
     slope = up * sigmoid * (1.0 + gate * (1.0 - sigmoid))
 
     def blocks(q):
         return pl.ds(pl.multiple_of(q * pair_block, pair_block), pair_block)
 
-    def send_slices(source, j):
+    def send_slices(source):
         for k in hops:
             remote(
                 a_buf.at[source, :, blocks(chip_at(k))],
                 s_all.at[chip, source],
-                s_ssem.at[j, k - 1],
-                s_rsem.at[k - 1],
+                slot_sem.at[0],
                 peer_at(k),
             )
 
-    send_slices(member, 0)
+    send_slices(member)
 
     mix_v[...] = jnp.concatenate(
-        [jnp.concatenate(ones[e * micro : (e + 1) * micro], axis=0) for e in range(window) for _ in range(2)],
+        [
+            jnp.concatenate(ones[e * micro : (e + 1) * micro], axis=0)
+            for e in range(window)
+            for _ in range(2)
+        ],
         axis=0,
     ).astype(BF16)
-    loads[5 + micro].wait()
-    x_copy.wait_recv()
+    pltpu.make_async_copy(x_par, x_par, x_sem.at[0]).wait()
     for k in range(chips):
         q = chip_at(k) if k else chip
         own = pl.ds(pl.multiple_of((q * 2 + core) * row_block, row_block), row_block)
@@ -529,94 +518,82 @@
         other = x_par[:, :, own].reshape(rows, row_block)
         xt_v[k] = jnp.concatenate([mine, other], axis=0).T
 
-    for j, source in enumerate(nearest):
-        a_arrival(source).wait_recv()
+    for j, k in enumerate(arriving):
+        source = member_at(k)
+        pltpu.make_async_copy(a_buf.at[source], a_buf.at[source], a_sem.at[k - 1]).wait()
         if j < n_exp - 2:
-            send_slices(source, j + 1)
+            send_slices(source)
     scaled = a_buf[...].reshape(rows, width)
     dhidden = dot(scaled, wd_v[...], 1, 1)
-    d_gate = (dhidden * slope).astype(BF16)
-    d_up = (dhidden * activated).astype(BF16)
-    d_all[0, :, :cols] = d_gate
-    d_all[0, :, cols:] = d_up
-    d_copy = remote(d_all.at[0], d_all.at[1], d_sem.at[0], d_sem.at[1], partner)
-    send_slices(nearest[-1], n_exp - 1)
-
-    returning = (dot(d_gate, wg_v[...], 1, 1) + dot(d_up, wu_v[...], 1, 1)).astype(BF16)
-    for h in range(n_exp):
-        r_send[h] = returning[h * part : (h + 1) * part]
-    r_copies = [
-        remote(
-            r_send.at[to], r_buf.at[member], r_ssem.at[k - 1], r_rsem.at[k - 1], {"expert": to}
-        )
-        for k, to in zip(range(n_exp - 1, 0, -1), order)
-    ]
-
-    d_copy.wait_recv()
+    d_all[0, :, :cols] = (dhidden * slope).astype(BF16)
+    d_all[0, :, cols:] = (dhidden * activated).astype(BF16)
+    remote(d_all.at[0], d_all.at[1], d_sem.at[0], partner)
+    send_slices(member_at(arriving[-1]))
+
+    def send_back():
+        returning = dot(d_all[0, :, :cols], wg_v[...], 1, 1) + dot(
+            d_all[0, :, cols:], wu_v[...], 1, 1
+        )
+        returning = returning.astype(BF16)
+        for h in range(n_exp):
+            r_send[h] = returning[h * part : (h + 1) * part]
+        for k in order:
+            to = member_at(k)
+            remote(r_send.at[to], r_buf.at[member], r_sem.at[0], {"expert": to}, False).start()
+
+    sent.append((n_exp - 1) * part * width)
+    returns_first = (core == 1) | (member != 0)
+
+    @pl.when(returns_first)
+    def _():
+        send_back()
+
+    pltpu.make_async_copy(d_all.at[1], d_all.at[1], d_sem.at[0]).wait()
     factors = d_all[...].reshape(2 * rows, 2 * cols)
-    far = dot(xt_v[3], factors, 1, 0).astype(BF16)
-    relays = []
-    for i, k in enumerate((1, 2)):
-        relay_send[i] = far[:, i * cols : (i + 1) * cols]
-        relays.append(
-            remote(
-                relay_send.at[i],
-                relay_buf.at[i],
-                relay_ssem.at[i],
-                relay_rsem.at[i],
-                peer_at(k),
-            )
-        )
-
-    def send_last(i, k, value):
+    def send_half(i, k, value, dst, sem):
         last_send[i] = value.astype(BF16)
-        return remote(
-            last_send.at[i], last_buf.at[i], last_ssem.at[i], last_rsem.at[i], peer_at(k)
-        )
-
+        remote(last_send.at[i], dst.at[i % 4], sem, peer_at(k))
+
+    far = dot(xt_v[3], factors, 1, 0)
+    send_half(4, 1, far[:, :cols], relay_buf, relay_sem.at[0])
+    send_half(5, 2, far[:, cols:], relay_buf, relay_sem.at[1])
     near = [dot(xt_v[k], factors, 1, 0) for k in (1, 2)]
-    last_copies = [
-        send_last(0, 1, near[0][:, :cols]),
-        send_last(1, 2, near[1][:, cols:]),
-    ]
+    send_half(0, 1, near[0][:, :cols], last_buf, last_sem.at[0])
+    send_half(1, 2, near[1][:, cols:], last_buf, last_sem.at[0])
     total = dot(xt_v[0], factors, 1, 0)
+    @pl.when(jnp.logical_not(returns_first))
+    def _():
+        send_back()
+
     r_buf[member] = r_send[member]
     s_all[chip] = a_buf[:, :, blocks(chip)]
-    relays[0].wait_recv()
-    last_copies.append(send_last(2, 2, near[1][:, :cols] + relay_buf[0].astype(F32)))
-    relays[1].wait_recv()
-    last_copies.append(send_last(3, 1, near[0][:, cols:] + relay_buf[1].astype(F32)))
-    for k in hops:
-        h_copies[k].wait_recv()
-        pltpu.make_async_remote_copy(
-            src_ref=s_all.at[chip],
-            dst_ref=s_all.at[chip_at(k)],
-            send_sem=s_ssem.at[0, k - 1],
-            recv_sem=s_rsem.at[k - 1],
-            device_id=peer_at(k),
-            device_id_type=MESH,
-        ).wait_recv()
+    for i, (k, value) in enumerate(((2, near[1][:, :cols]), (1, near[0][:, cols:]))):
+        pltpu.make_async_copy(relay_buf.at[i], relay_buf.at[i], relay_sem.at[i]).wait()
+        send_half(
+            2 + i, k, value + relay_buf[i].astype(F32), last_buf, last_sem.at[1]
+        )
+    others = (chips - 1) * (rows * cols + rows * pair_block)
+    arrivals(others // width, slot_sem.at[0]).wait()
     slots = chips * rows
     down = dot(s_all[...].reshape(slots, pair_block), h_all[...].reshape(slots, cols), 0, 0)
     down_v[0] = down[:row_block]
     down_v[1] = down[row_block:]
-    down_copy = remote(down_v.at[1 - core], down_buf, down_sem.at[0], down_sem.at[1], partner)
-
-    for copy in r_copies:
-        copy.wait_recv()
+    remote(down_v.at[1 - core], down_buf, down_sem.at[0], partner)
+
+    arrivals((n_exp - 1) * part, r_sem.at[0]).wait()
     gin_ref[...] = dot(mix_v[...], r_buf[...].reshape(rows, width), 0, 0).astype(BF16)
 
     factor = 1.0 / (micro * n_dp)
-    down_copy.wait_recv()
+    pltpu.make_async_copy(down_buf, down_buf, down_sem.at[0]).wait()
     gd_ref[...] = (down_v[core] + down_buf[...]) * factor
-    for copy in last_copies:
-        copy.wait_recv()
-    gates = total[:, :cols] + last_buf[0].astype(F32) + last_buf[2].astype(F32)
-    ups = total[:, cols:] + last_buf[1].astype(F32) + last_buf[3].astype(F32)
-    gg_ref[...] = gates * factor
-    gu_ref[...] = ups * factor
-    for copy in started:
-        copy.wait_send()
+    halves = 2 * row_block * cols // width
+    arrivals(halves, last_sem.at[0]).wait()
+    gg_ref[...] = (total[:, :cols] + last_buf[0].astype(F32)) * factor
+    gu_ref[...] = (total[:, cols:] + last_buf[1].astype(F32)) * factor
+    arrivals(halves, last_sem.at[1]).wait()
+    gg_ref[...] = gg_ref[...] + last_buf[2].astype(F32) * factor
+    gu_ref[...] = gu_ref[...] + last_buf[3].astype(F32) * factor
+    arrivals(sum(sent) // width, sent_sem.at[0]).wait()
 
 
 def settle(*refs):
@@ -676,29 +653,23 @@
             pltpu.VMEM((rows, tokens), BF16),
             pltpu.VMEM((2, rows, 2 * cols), BF16),
             pltpu.VMEM((2, row_block, cols), BF16),
-            pltpu.VMEM((2, row_block, cols), BF16),
-            pltpu.VMEM((4, row_block, cols), BF16),
+            pltpu.VMEM((6, row_block, cols), BF16),
             pltpu.VMEM((4, row_block, cols), BF16),
             pltpu.VMEM((chips, n_exp, part, 2 * row_block), BF16),
             pltpu.VMEM((chips, rows, cols), BF16),
             pltpu.VMEM((2, row_block, cols), F32),
             pltpu.VMEM((row_block, cols), F32),
-            dma((6 + micro,)),
+            pltpu.VMEM((width, width), BF16),
+            dma((4,)),
+            dma((1,)),
             dma((n_exp - 1,)),
-            dma((n_exp,)),
-            dma((n_exp - 1,)),
-            dma((n_exp - 1,)),
+            dma((1,)),
+            dma((1,)),
+            dma((1,)),
             dma((2,)),
             dma((2,)),
-            dma((2,)),
-            dma((2,)),
-            dma((4,)),
-            dma((4,)),
-            dma((n_exp, chips - 1)),
-            dma((chips - 1,)),
-            dma((chips - 1,)),
-            dma((chips - 1,)),
-            dma((2,)),
+            dma((1,)),
+            dma((1,)),
         ],
         compiler_params=pltpu.CompilerParams(collective_id=0, has_side_effects=True),
     )(

time: 23.8 us -> 21.4 us (0.90)
  Pallas kernels: 22.9 us -> 20.6 us
    pallas_call x1, Pallas kernels: 21.9 us -> 19.6 us  [pooled_call(): pl.pallas_call(functools.partial(pooled_kernel, micro, n_exp, n_dp), out_...]
where the time goes in v3:
time: 21.4 us; the launch traced here: 21.2 us
  Pallas kernels  20.6 us (96%)
  between operations  0.64 us (3%)
    pallas_call x1, Pallas kernels, pooled_call(): pl.pallas_call(functools.partial(pooled_kernel, micro, n_exp, n_dp), out_...  19.6 us
    pallas_call x1, Pallas kernels, settled(): pl.pallas_call(settle, out_shape=tuple((jax.ShapeDtypeStruct(a.shape, a.d...  0.95 us

profile of v3, /device:TPU:0, one launch (start us, length us, event | category | flops | bytes accessed | tf_op | source)
XLA Modules:
  0.0 21.2 jit_solution(9257477671372663704)
XLA Ops:
  0.6 19.6 %shard_map.102 = (bf16[256,1024]{1,0:T(8,128)(2,1)S(1)}, f32[128,256]{1,0:T(8,128)S(1)}, f32[128,256]{1,0:T(8,128)S(1)}, f32[128,256]{1,0:T(8,128)S(1)}) custom-call(s32[4,8,64]{2,1,0:T(8,128)} %bitcast.7, bf16[4,8,64]{2,1,0:T(8,128)(2,1)} %bitcast.8, bf16[256,1024]{1,0:T(8,128)(2,1)} %bitcast.5, bf16[4,4,8,1024]{3,2,1,0:T(8,128)(2,1)} %bitcast.6, ...), custom_call_target="tpu_custom_call" | custom-call | tf_op jit(solution)/shard_map/pallas_call | solution.py:634
  20.2 1.0 %shard_map.103 = (bf16[256,1024]{1,0:T(8,128)(2,1)}, f32[128,256]{1,0:T(8,128)}, f32[128,256]{1,0:T(8,128)}, f32[128,256]{1,0:T(8,128)}) custom-call(bf16[256,1024]{1,0:T(8,128)(2,1)S(1)} %get-tuple-element.12.refs_0_, f32[128,256]{1,0:T(8,128)S(1)} %get-tuple-element.13.refs_1_, f32[128,256]{1,0:T(8,128)S(1)} %get-tuple-element.14.refs_2_, ...), custom_call_target="tpu_custom_call" | custom-call | tf_op jit(solution)/shard_map/pallas_call | solution.py:613

commit v4 on v3

--- a/solution.py
+++ b/solution.py
@@ -378,15 +378,6 @@
     def peer_at(k):
         return {"dp": chip_at(k) * 2 + core}
 
-    barrier = pltpu.get_barrier_semaphore()
-    for k in range(n_exp - 1, 0, -1):
-        pl.semaphore_signal(
-            barrier, inc=1, device_id={"expert": flipped(member, k)}, device_id_type=MESH
-        )
-    for k in hops:
-        pl.semaphore_signal(barrier, inc=1, device_id=peer_at(k), device_id_type=MESH)
-    pl.semaphore_signal(barrier, inc=1, device_id=partner, device_id_type=MESH)
-
     loads = [
         pltpu.make_async_copy(src, dst, load_sem.at[min(i, 3)])
         for i, (src, dst) in enumerate(
@@ -401,15 +392,24 @@
             )
         )
     ]
-    for load in loads:
+    for load in loads[:3]:
         load.start()
+
+    barrier = pltpu.get_barrier_semaphore()
+    for k in range(n_exp - 1, 0, -1):
+        pl.semaphore_signal(
+            barrier, inc=1, device_id={"expert": flipped(member, k)}, device_id_type=MESH
+        )
+    for k in hops:
+        pl.semaphore_signal(barrier, inc=1, device_id=peer_at(k), device_id_type=MESH)
+    pl.semaphore_signal(barrier, inc=1, device_id=partner, device_id_type=MESH)
 
     def arrivals(size, sem):
         return pltpu.make_async_copy(sized.at[pl.ds(0, size)], sized.at[pl.ds(0, size)], sem)
 
     sent = []
 
-    def remote(src, dst, sem, device, start=True):
+    def remote(src, dst, sem, device, counted=True):
         copy = pltpu.make_async_remote_copy(
             src_ref=src,
             dst_ref=dst,
@@ -418,13 +418,12 @@
             device_id=device,
             device_id_type=MESH,
         )
-        if start:
-            copy.start()
+        copy.start()
+        if counted:
             bulk = 1
             for n in src.shape:
                 bulk *= n
             sent.append(bulk * (2 if src.dtype == F32 else 1))
-        return copy
 
     pad = max(window, 8)
     expert_row = lax.broadcasted_iota(jnp.int32, (pad, tokens), 0)
@@ -455,6 +454,8 @@
     picking = jnp.concatenate(scales, axis=0).astype(BF16)
 
     loads[2].wait()
+    for load in loads[3:]:
+        load.start()
     sending = dot(picking, go_v[...], 1, 0).astype(BF16)
     for e in range(window):
         a_send[e] = sending[e * part : (e + 1) * part]
@@ -491,13 +492,14 @@
     def blocks(q):
         return pl.ds(pl.multiple_of(q * pair_block, pair_block), pair_block)
 
-    def send_slices(source):
+    def send_slices(source, counted=True):
         for k in hops:
             remote(
                 a_buf.at[source, :, blocks(chip_at(k))],
                 s_all.at[chip, source],
                 slot_sem.at[0],
                 peer_at(k),
+                counted,
             )
 
     send_slices(member)
@@ -528,7 +530,12 @@
     d_all[0, :, :cols] = (dhidden * slope).astype(BF16)
     d_all[0, :, cols:] = (dhidden * activated).astype(BF16)
     remote(d_all.at[0], d_all.at[1], d_sem.at[0], partner)
-    send_slices(member_at(arriving[-1]))
+
+    @pl.when(core == 1)
+    def _():
+        send_slices(member_at(arriving[-1]), False)
+
+    sent.append((chips - 1) * part * pair_block)
 
     def send_back():
         returning = dot(d_all[0, :, :cols], wg_v[...], 1, 1) + dot(
@@ -537,9 +544,9 @@
         returning = returning.astype(BF16)
         for h in range(n_exp):
             r_send[h] = returning[h * part : (h + 1) * part]
-        for k in order:
+        for k in (3 - inner, 2 + inner, 1):
             to = member_at(k)
-            remote(r_send.at[to], r_buf.at[member], r_sem.at[0], {"expert": to}, False).start()
+            remote(r_send.at[to], r_buf.at[member], r_sem.at[0], {"expert": to}, False)
 
     sent.append((n_exp - 1) * part * width)
     returns_first = (core == 1) | (member != 0)
@@ -555,8 +562,22 @@
         remote(last_send.at[i], dst.at[i % 4], sem, peer_at(k))
 
     far = dot(xt_v[3], factors, 1, 0)
-    send_half(4, 1, far[:, :cols], relay_buf, relay_sem.at[0])
-    send_half(5, 2, far[:, cols:], relay_buf, relay_sem.at[1])
+    last_send[4] = far[:, :cols].astype(BF16)
+    last_send[5] = far[:, cols:].astype(BF16)
+    strips = [pl.ds(c * row_block // 2, row_block // 2) for c in range(2)]
+    for c, strip in enumerate(strips):
+        for i in range(2):
+            remote(
+                last_send.at[4 + i, strip],
+                relay_buf.at[i, strip],
+                relay_sem.at[i, c],
+                peer_at(1 + i),
+            )
+
+    @pl.when(core == 0)
+    def _():
+        send_slices(member_at(arriving[-1]), False)
+
     near = [dot(xt_v[k], factors, 1, 0) for k in (1, 2)]
     send_half(0, 1, near[0][:, :cols], last_buf, last_sem.at[0])
     send_half(1, 2, near[1][:, cols:], last_buf, last_sem.at[0])
@@ -567,11 +588,19 @@
 
     r_buf[member] = r_send[member]
     s_all[chip] = a_buf[:, :, blocks(chip)]
-    for i, (k, value) in enumerate(((2, near[1][:, :cols]), (1, near[0][:, cols:]))):
-        pltpu.make_async_copy(relay_buf.at[i], relay_buf.at[i], relay_sem.at[i]).wait()
-        send_half(
-            2 + i, k, value + relay_buf[i].astype(F32), last_buf, last_sem.at[1]
-        )
+    own_term = (near[1][:, :cols], near[0][:, cols:])
+    for c, strip in enumerate(strips):
+        for i in range(2):
+            piece = relay_buf.at[i, strip]
+            pltpu.make_async_copy(piece, piece, relay_sem.at[i, c]).wait()
+            value = own_term[i][c * row_block // 2 : (c + 1) * row_block // 2]
+            last_send[2 + i, strip] = (value + piece[...].astype(F32)).astype(BF16)
+            remote(
+                last_send.at[2 + i, strip],
+                last_buf.at[2 + i, strip],
+                last_sem.at[1],
+                peer_at(2 - i),
+            )
     others = (chips - 1) * (rows * cols + rows * pair_block)
     arrivals(others // width, slot_sem.at[0]).wait()
     slots = chips * rows
@@ -666,7 +695,7 @@
             dma((1,)),
             dma((1,)),
             dma((1,)),
-            dma((2,)),
+            dma((2, 2)),
             dma((2,)),
             dma((1,)),
             dma((1,)),

time: 21.4 us -> 20.8 us (0.972)
  Pallas kernels: 20.6 us -> 19.9 us
    pallas_call x1, Pallas kernels: 19.6 us -> 19 us  [pooled_call(): pl.pallas_call(functools.partial(pooled_kernel, micro, n_exp, n_dp), out_...]
where the time goes in v4:
time: 20.8 us; the launch traced here: 20.5 us
  Pallas kernels  19.9 us (96%)
  between operations  0.64 us (3%)
    pallas_call x1, Pallas kernels, pooled_call(): pl.pallas_call(functools.partial(pooled_kernel, micro, n_exp, n_dp), out_...  19 us
    pallas_call x1, Pallas kernels, settled(): pl.pallas_call(settle, out_shape=tuple((jax.ShapeDtypeStruct(a.shape, a.d...  0.95 us

profile of v4, /device:TPU:0, one launch (start us, length us, event | category | flops | bytes accessed | tf_op | source)
XLA Modules:
  0.0 20.5 jit_solution(15202987224093976794)
XLA Ops:
  0.6 19.0 %shard_map.102 = (bf16[256,1024]{1,0:T(8,128)(2,1)S(1)}, f32[128,256]{1,0:T(8,128)S(1)}, f32[128,256]{1,0:T(8,128)S(1)}, f32[128,256]{1,0:T(8,128)S(1)}) custom-call(s32[4,8,64]{2,1,0:T(8,128)} %bitcast.7, bf16[4,8,64]{2,1,0:T(8,128)(2,1)} %bitcast.8, bf16[256,1024]{1,0:T(8,128)(2,1)} %bitcast.5, bf16[4,4,8,1024]{3,2,1,0:T(8,128)(2,1)} %bitcast.6, ...), custom_call_target="tpu_custom_call" | custom-call | tf_op jit(solution)/shard_map/pallas_call | solution.py:663
  19.6 1.0 %shard_map.103 = (bf16[256,1024]{1,0:T(8,128)(2,1)}, f32[128,256]{1,0:T(8,128)}, f32[128,256]{1,0:T(8,128)}, f32[128,256]{1,0:T(8,128)}) custom-call(bf16[256,1024]{1,0:T(8,128)(2,1)S(1)} %get-tuple-element.12.refs_0_, f32[128,256]{1,0:T(8,128)S(1)} %get-tuple-element.13.refs_1_, f32[128,256]{1,0:T(8,128)S(1)} %get-tuple-element.14.refs_2_, ...), custom_call_target="tpu_custom_call" | custom-call | tf_op jit(solution)/shard_map/pallas_call | solution.py:642

commit v5 on v4

--- a/solution.py
+++ b/solution.py
@@ -340,6 +340,7 @@
     relay_buf,
     last_send,
     last_buf,
+    sums_send,
     s_all,
     h_all,
     down_v,
@@ -355,6 +356,7 @@
     last_sem,
     slot_sem,
     down_sem,
+    turn_sem,
 ):
     member = lax.axis_index("expert")
     replica = lax.axis_index("dp")
@@ -375,8 +377,8 @@
     def chip_at(k):
         return flipped(chip, k)
 
-    def peer_at(k):
-        return {"dp": chip_at(k) * 2 + core}
+    def peer_at(k, side=core):
+        return {"dp": chip_at(k) * 2 + side}
 
     loads = [
         pltpu.make_async_copy(src, dst, load_sem.at[min(i, 3)])
@@ -403,17 +405,19 @@
     for k in hops:
         pl.semaphore_signal(barrier, inc=1, device_id=peer_at(k), device_id_type=MESH)
     pl.semaphore_signal(barrier, inc=1, device_id=partner, device_id_type=MESH)
+    for k in (1, 2):
+        pl.semaphore_signal(barrier, inc=1, device_id=peer_at(k, 1 - core), device_id_type=MESH)
 
     def arrivals(size, sem):
         return pltpu.make_async_copy(sized.at[pl.ds(0, size)], sized.at[pl.ds(0, size)], sem)
 
     sent = []
 
-    def remote(src, dst, sem, device, counted=True):
+    def remote(src, dst, sem, device, counted=True, group=0):
         copy = pltpu.make_async_remote_copy(
             src_ref=src,
             dst_ref=dst,
-            send_sem=sent_sem.at[0],
+            send_sem=sent_sem.at[group],
             recv_sem=sem,
             device_id=device,
             device_id_type=MESH,
@@ -459,11 +463,12 @@
     sending = dot(picking, go_v[...], 1, 0).astype(BF16)
     for e in range(window):
         a_send[e] = sending[e * part : (e + 1) * part]
-    pl.semaphore_wait(barrier, n_exp - 1 + chips)
+    pl.semaphore_wait(barrier, n_exp - 1 + chips + 2)
 
     inner = jnp.where((member == 0) | (member == n_exp - 1), 0, 1)
-    order = [1 + inner, 3, 2 - inner]
-    arriving = [1, 2 + inner, 3 - inner]
+    outer = (1 - inner) * (1 - core)
+    order = [1 + inner + 2 * outer, 3 - 2 * outer, 2 - inner]
+    arriving = [1, 3, 2]
 
     def member_at(k):
         low, high = lax.rem(k, 2), lax.div(k, 2)
@@ -513,12 +518,13 @@
         axis=0,
     ).astype(BF16)
     pltpu.make_async_copy(x_par, x_par, x_sem.at[0]).wait()
-    for k in range(chips):
+    for j in range(chips + 2):
+        k, side = (j, core) if j < chips else (j - chips + 1, 0)
         q = chip_at(k) if k else chip
-        own = pl.ds(pl.multiple_of((q * 2 + core) * row_block, row_block), row_block)
+        own = pl.ds(pl.multiple_of((q * 2 + side) * row_block, row_block), row_block)
         mine = x_v[:, :, own].reshape(rows, row_block)
         other = x_par[:, :, own].reshape(rows, row_block)
-        xt_v[k] = jnp.concatenate([mine, other], axis=0).T
+        xt_v[j] = jnp.concatenate([mine, other], axis=0).T
 
     for j, k in enumerate(arriving):
         source = member_at(k)
@@ -537,6 +543,9 @@
 
     sent.append((chips - 1) * part * pair_block)
 
+    def send_rows(to):
+        remote(r_send.at[to], r_buf.at[member], r_sem.at[0], {"expert": to}, False)
+
     def send_back():
         returning = dot(d_all[0, :, :cols], wg_v[...], 1, 1) + dot(
             d_all[0, :, cols:], wu_v[...], 1, 1
@@ -544,9 +553,13 @@
         returning = returning.astype(BF16)
         for h in range(n_exp):
             r_send[h] = returning[h * part : (h + 1) * part]
-        for k in (3 - inner, 2 + inner, 1):
-            to = member_at(k)
-            remote(r_send.at[to], r_buf.at[member], r_sem.at[0], {"expert": to}, False)
+        for k in (3 - inner, 1):
+            send_rows(member_at(k))
+
+        @pl.when(core == 0)
+        def _():
+            send_rows(member_at(2 + inner))
+
 
     sent.append((n_exp - 1) * part * width)
     returns_first = (core == 1) | (member != 0)
@@ -557,30 +570,27 @@
 
     pltpu.make_async_copy(d_all.at[1], d_all.at[1], d_sem.at[0]).wait()
     factors = d_all[...].reshape(2 * rows, 2 * cols)
-    def send_half(i, k, value, dst, sem):
-        last_send[i] = value.astype(BF16)
-        remote(last_send.at[i], dst.at[i % 4], sem, peer_at(k))
-
+    half = row_block // 2
+    strips = [pl.ds(c * half, half) for c in range(2)]
     far = dot(xt_v[3], factors, 1, 0)
-    last_send[4] = far[:, :cols].astype(BF16)
-    last_send[5] = far[:, cols:].astype(BF16)
-    strips = [pl.ds(c * row_block // 2, row_block // 2) for c in range(2)]
+    for i in range(2):
+        last_send[4 + i] = far[:, i * cols : (i + 1) * cols].astype(BF16)
     for c, strip in enumerate(strips):
         for i in range(2):
             remote(
                 last_send.at[4 + i, strip],
-                relay_buf.at[i, strip],
-                relay_sem.at[i, c],
-                peer_at(1 + i),
+                relay_buf.at[1 - core, i, strip],
+                relay_sem.at[1 - core, c],
+                peer_at(1 + i, 1),
             )
 
-    @pl.when(core == 0)
+    @pl.when(core == 1)
     def _():
-        send_slices(member_at(arriving[-1]), False)
+        pl.semaphore_signal(turn_sem, inc=1, device_id=partner, device_id_type=MESH)
 
     near = [dot(xt_v[k], factors, 1, 0) for k in (1, 2)]
-    send_half(0, 1, near[0][:, :cols], last_buf, last_sem.at[0])
-    send_half(1, 2, near[1][:, cols:], last_buf, last_sem.at[0])
+    last_send[0] = near[0][:, :cols].astype(BF16)
+    last_send[1] = near[1][:, cols:].astype(BF16)
     total = dot(xt_v[0], factors, 1, 0)
     @pl.when(jnp.logical_not(returns_first))
     def _():
@@ -588,19 +598,42 @@
 
     r_buf[member] = r_send[member]
     s_all[chip] = a_buf[:, :, blocks(chip)]
-    own_term = (near[1][:, :cols], near[0][:, cols:])
-    for c, strip in enumerate(strips):
-        for i in range(2):
-            piece = relay_buf.at[i, strip]
-            pltpu.make_async_copy(piece, piece, relay_sem.at[i, c]).wait()
-            value = own_term[i][c * row_block // 2 : (c + 1) * row_block // 2]
-            last_send[2 + i, strip] = (value + piece[...].astype(F32)).astype(BF16)
-            remote(
-                last_send.at[2 + i, strip],
-                last_buf.at[2 + i, strip],
-                last_sem.at[1],
-                peer_at(2 - i),
-            )
+
+    @pl.when(core == 0)
+    def _():
+        pl.semaphore_wait(turn_sem, 1)
+
+
+    @pl.when(core == 0)
+    def _():
+        send_slices(member_at(arriving[-1]), False)
+
+    for i in range(2):
+        remote(last_send.at[i], last_buf.at[i], last_sem.at[0], peer_at(1 + i))
+    @pl.when(core == 1)
+    def _():
+        extra = [
+            dot(xt_v[chips + 1], factors[:, :cols], 1, 0),
+            dot(xt_v[chips], factors[:, cols:], 1, 0),
+        ]
+        terms = [[near[1][:, :cols], near[0][:, cols:]], extra]
+        for side in (1, 0):
+            for c, strip in enumerate(strips):
+                arrivals(2 * half * cols // width, relay_sem.at[side, c]).wait()
+                if side == 1 and c == 0:
+                    send_rows(member_at(2 + inner))
+                for i in range(2):
+                    value = terms[side][i][c * half : (c + 1) * half]
+                    value = value + relay_buf[side, i, strip].astype(F32)
+                    sums_send[side, i, strip] = value.astype(BF16)
+                    remote(
+                        sums_send.at[side, i, strip],
+                        last_buf.at[2 + i, strip],
+                        last_sem.at[1],
+                        peer_at(2 - i, 1 - side),
+                        False,
+                        1,
+                    )
     others = (chips - 1) * (rows * cols + rows * pair_block)
     arrivals(others // width, slot_sem.at[0]).wait()
     slots = chips * rows
@@ -622,29 +655,34 @@
     arrivals(halves, last_sem.at[1]).wait()
     gg_ref[...] = gg_ref[...] + last_buf[2].astype(F32) * factor
     gu_ref[...] = gu_ref[...] + last_buf[3].astype(F32) * factor
+
+    @pl.when(core == 1)
+    def _():
+        arrivals(4 * row_block * cols // width, sent_sem.at[1]).wait()
+
     arrivals(sum(sent) // width, sent_sem.at[0]).wait()
 
 
 def settle(*refs):
-    count = len(refs) // 2
-    sem = refs[-1]
-    copies = [
-        pltpu.make_async_copy(refs[i], refs[count + i], sem.at[i]) for i in range(count)
-    ]
-    for copy in copies:
-        copy.start()
-    for copy in copies:
-        copy.wait()
+    count = len(refs) // 2 - 1
+    sized, sem = refs[-2:]
+    for i in range(count):
+        pltpu.make_async_copy(refs[i], refs[count + i], sem.at[0]).start()
+    pltpu.make_async_copy(sized, sized, sem.at[0]).wait()
 
 
 def settled(arrays):
     anywhere = pl.BlockSpec(memory_space=pl.ANY)
+    words = sum(a.size * a.dtype.itemsize // 2 for a in arrays)
     return pl.pallas_call(
         settle,
         out_shape=tuple(jax.ShapeDtypeStruct(a.shape, a.dtype) for a in arrays),
         in_specs=[pl.BlockSpec(memory_space=pltpu.VMEM)] * len(arrays),
         out_specs=(anywhere,) * len(arrays),
-        scratch_shapes=[pltpu.SemaphoreType.DMA((len(arrays),))],
+        scratch_shapes=[
+            pltpu.VMEM((words // arrays[0].shape[1], arrays[0].shape[1]), BF16),
+            pltpu.SemaphoreType.DMA((1,)),
+        ],
     )(*[pltpu.with_memory_space_constraint(a, pltpu.VMEM) for a in arrays])
 
 
@@ -671,7 +709,7 @@
             pltpu.VMEM((tokens, width), BF16),
             pltpu.VMEM((n_exp, part, width), BF16),
             pltpu.VMEM((n_exp, part, width), BF16),
-            pltpu.VMEM((chips, row_block, 2 * rows), BF16),
+            pltpu.VMEM((chips + 2, row_block, 2 * rows), BF16),
             pltpu.VMEM((width, cols), BF16),
             pltpu.VMEM((width, cols), BF16),
             pltpu.VMEM((cols, width), BF16),
@@ -681,16 +719,17 @@
             pltpu.VMEM((n_exp, part, width), BF16),
             pltpu.VMEM((rows, tokens), BF16),
             pltpu.VMEM((2, rows, 2 * cols), BF16),
-            pltpu.VMEM((2, row_block, cols), BF16),
+            pltpu.VMEM((2, 2, row_block, cols), BF16),
             pltpu.VMEM((6, row_block, cols), BF16),
             pltpu.VMEM((4, row_block, cols), BF16),
+            pltpu.VMEM((2, 2, row_block, cols), BF16),
             pltpu.VMEM((chips, n_exp, part, 2 * row_block), BF16),
             pltpu.VMEM((chips, rows, cols), BF16),
             pltpu.VMEM((2, row_block, cols), F32),
             pltpu.VMEM((row_block, cols), F32),
             pltpu.VMEM((width, width), BF16),
             dma((4,)),
-            dma((1,)),
+            dma((2,)),
             dma((n_exp - 1,)),
             dma((1,)),
             dma((1,)),
@@ -699,6 +738,7 @@
             dma((2,)),
             dma((1,)),
             dma((1,)),
+            pltpu.SemaphoreType.REGULAR,
         ],
         compiler_params=pltpu.CompilerParams(collective_id=0, has_side_effects=True),
     )(

time: 20.8 us -> 20.5 us (0.986)
  Pallas kernels: 19.9 us -> 19.6 us
    pallas_call x1, Pallas kernels: 19 us -> 18.7 us  [pooled_call(): pl.pallas_call(functools.partial(pooled_kernel, micro, n_exp, n_dp), out_...]
where the time goes in v5:
time: 20.5 us; the launch traced here: 20.2 us
  Pallas kernels  19.6 us (96%)
  between operations  0.64 us (3%)
    pallas_call x1, Pallas kernels, pooled_call(): pl.pallas_call(functools.partial(pooled_kernel, micro, n_exp, n_dp), out_...  18.7 us
    pallas_call x1, Pallas kernels, settled(): pl.pallas_call(settle, out_shape=tuple((jax.ShapeDtypeStruct(a.shape, a.d...  0.92 us

profile of v5, /device:TPU:0, one launch (start us, length us, event | category | flops | bytes accessed | tf_op | source)
XLA Modules:
  0.0 20.2 jit_solution(7680616775194428159)
XLA Ops:
  0.6 18.7 %shard_map.102 = (bf16[256,1024]{1,0:T(8,128)(2,1)S(1)}, f32[128,256]{1,0:T(8,128)S(1)}, f32[128,256]{1,0:T(8,128)S(1)}, f32[128,256]{1,0:T(8,128)S(1)}) custom-call(s32[4,8,64]{2,1,0:T(8,128)} %bitcast.7, bf16[4,8,64]{2,1,0:T(8,128)(2,1)} %bitcast.8, bf16[256,1024]{1,0:T(8,128)(2,1)} %bitcast.5, bf16[4,4,8,1024]{3,2,1,0:T(8,128)(2,1)} %bitcast.6, ...), custom_call_target="tpu_custom_call" | custom-call | tf_op jit(solution)/shard_map/pallas_call | solution.py:701
  19.3 0.9 %shard_map.103 = (bf16[256,1024]{1,0:T(8,128)(2,1)}, f32[128,256]{1,0:T(8,128)}, f32[128,256]{1,0:T(8,128)}, f32[128,256]{1,0:T(8,128)}) custom-call(bf16[256,1024]{1,0:T(8,128)(2,1)S(1)} %get-tuple-element.12.refs_0_, f32[128,256]{1,0:T(8,128)S(1)} %get-tuple-element.13.refs_1_, f32[128,256]{1,0:T(8,128)S(1)} %get-tuple-element.14.refs_2_, ...), custom_call_target="tpu_custom_call" | custom-call | tf_op jit(solution)/shard_map/pallas_call | solution.py:677

commit v6 on v5

--- a/solution.py
+++ b/solution.py
@@ -331,6 +331,8 @@
     wg_v,
     wu_v,
     wd_v,
+    wdt_v,
+    wgt_v,
     a_send,
     a_buf,
     r_send,
@@ -517,6 +519,9 @@
         ],
         axis=0,
     ).astype(BF16)
+    wdt_v[...] = wd_v[...].T
+    wgt_v[:cols] = wg_v[...].T
+    wgt_v[cols:] = wu_v[...].T
     pltpu.make_async_copy(x_par, x_par, x_sem.at[0]).wait()
     for j in range(chips + 2):
         k, side = (j, core) if j < chips else (j - chips + 1, 0)
@@ -532,7 +537,7 @@
         if j < n_exp - 2:
             send_slices(source)
     scaled = a_buf[...].reshape(rows, width)
-    dhidden = dot(scaled, wd_v[...], 1, 1)
+    dhidden = dot(scaled, wdt_v[...], 1, 0)
     d_all[0, :, :cols] = (dhidden * slope).astype(BF16)
     d_all[0, :, cols:] = (dhidden * activated).astype(BF16)
     remote(d_all.at[0], d_all.at[1], d_sem.at[0], partner)
@@ -547,9 +552,7 @@
         remote(r_send.at[to], r_buf.at[member], r_sem.at[0], {"expert": to}, False)
 
     def send_back():
-        returning = dot(d_all[0, :, :cols], wg_v[...], 1, 1) + dot(
-            d_all[0, :, cols:], wu_v[...], 1, 1
-        )
+        returning = dot(d_all[0], wgt_v[...], 1, 0)
         returning = returning.astype(BF16)
         for h in range(n_exp):
             r_send[h] = returning[h * part : (h + 1) * part]
@@ -629,7 +632,7 @@
                     remote(
                         sums_send.at[side, i, strip],
                         last_buf.at[2 + i, strip],
-                        last_sem.at[1],
+                        last_sem.at[1 + c],
                         peer_at(2 - i, 1 - side),
                         False,
                         1,
@@ -652,9 +655,10 @@
     arrivals(halves, last_sem.at[0]).wait()
     gg_ref[...] = (total[:, :cols] + last_buf[0].astype(F32)) * factor
     gu_ref[...] = (total[:, cols:] + last_buf[1].astype(F32)) * factor
-    arrivals(halves, last_sem.at[1]).wait()
-    gg_ref[...] = gg_ref[...] + last_buf[2].astype(F32) * factor
-    gu_ref[...] = gu_ref[...] + last_buf[3].astype(F32) * factor
+    for c, strip in enumerate(strips):
+        arrivals(halves // 2, last_sem.at[1 + c]).wait()
+        gg_ref[strip] = gg_ref[strip] + last_buf[2, strip].astype(F32) * factor
+        gu_ref[strip] = gu_ref[strip] + last_buf[3, strip].astype(F32) * factor
 
     @pl.when(core == 1)
     def _():
@@ -667,7 +671,10 @@
     count = len(refs) // 2 - 1
     sized, sem = refs[-2:]
     for i in range(count):
-        pltpu.make_async_copy(refs[i], refs[count + i], sem.at[0]).start()
+        strip = refs[i].shape[0] // 4
+        for c in range(4):
+            span = pl.ds(c * strip, strip)
+            pltpu.make_async_copy(refs[i].at[span], refs[count + i].at[span], sem.at[0]).start()
     pltpu.make_async_copy(sized, sized, sem.at[0]).wait()
 
 
@@ -713,6 +720,8 @@
             pltpu.VMEM((width, cols), BF16),
             pltpu.VMEM((width, cols), BF16),
             pltpu.VMEM((cols, width), BF16),
+            pltpu.VMEM((width, cols), BF16),
+            pltpu.VMEM((2 * cols, width), BF16),
             pltpu.VMEM((n_exp // 2, part, width), BF16),
             pltpu.VMEM((n_exp, part, width), BF16),
             pltpu.VMEM((n_exp, part, width), BF16),
@@ -735,7 +744,7 @@
             dma((1,)),
             dma((1,)),
             dma((2, 2)),
-            dma((2,)),
+            dma((3,)),
             dma((1,)),
             dma((1,)),
             pltpu.SemaphoreType.REGULAR,

time: 20.5 us -> 20.4 us (level)
  no operation moved by 1% of the time
where the time goes in v6:
time: 20.4 us; the launch traced here: 20.1 us
  Pallas kernels  19.5 us (96%)
  between operations  0.64 us (3%)
    pallas_call x1, Pallas kernels, pooled_call(): pl.pallas_call(functools.partial(pooled_kernel, micro, n_exp, n_dp), out_...  18.6 us
    pallas_call x1, Pallas kernels, settled(): pl.pallas_call(settle, out_shape=tuple((jax.ShapeDtypeStruct(a.shape, a.d...  0.91 us

profile of v6, /device:TPU:0, one launch (start us, length us, event | category | flops | bytes accessed | tf_op | source)
XLA Modules:
  0.0 20.1 jit_solution(9387094182228587423)
XLA Ops:
  0.6 18.6 %shard_map.102 = (bf16[256,1024]{1,0:T(8,128)(2,1)S(1)}, f32[128,256]{1,0:T(8,128)S(1)}, f32[128,256]{1,0:T(8,128)S(1)}, f32[128,256]{1,0:T(8,128)S(1)}) custom-call(s32[4,8,64]{2,1,0:T(8,128)} %bitcast.7, bf16[4,8,64]{2,1,0:T(8,128)(2,1)} %bitcast.8, bf16[256,1024]{1,0:T(8,128)(2,1)} %bitcast.5, bf16[4,4,8,1024]{3,2,1,0:T(8,128)(2,1)} %bitcast.6, ...), custom_call_target="tpu_custom_call" | custom-call | tf_op jit(solution)/shard_map/pallas_call | solution.py:708
  19.2 0.9 %shard_map.103 = (bf16[256,1024]{1,0:T(8,128)(2,1)}, f32[128,256]{1,0:T(8,128)}, f32[128,256]{1,0:T(8,128)}, f32[128,256]{1,0:T(8,128)}) custom-call(bf16[256,1024]{1,0:T(8,128)(2,1)S(1)} %get-tuple-element.12.refs_0_, f32[128,256]{1,0:T(8,128)S(1)} %get-tuple-element.13.refs_1_, f32[128,256]{1,0:T(8,128)S(1)} %get-tuple-element.14.refs_2_, ...), custom_call_target="tpu_custom_call" | custom-call | tf_op jit(solution)/shard_map/pallas_call | solution.py:684

commit v7 on v6

--- a/solution.py
+++ b/solution.py
@@ -611,8 +611,12 @@
     def _():
         send_slices(member_at(arriving[-1]), False)
 
-    for i in range(2):
-        remote(last_send.at[i], last_buf.at[i], last_sem.at[0], peer_at(1 + i))
+    @pl.when(core == 0)
+    def _():
+        for i in range(2):
+            remote(last_send.at[i], last_buf.at[i], last_sem.at[0], peer_at(1 + i), False)
+
+    sent.append(2 * row_block * cols)
     @pl.when(core == 1)
     def _():
         extra = [
@@ -625,6 +629,10 @@
                 arrivals(2 * half * cols // width, relay_sem.at[side, c]).wait()
                 if side == 1 and c == 0:
                     send_rows(member_at(2 + inner))
+                    for i in range(2):
+                        remote(
+                            last_send.at[i], last_buf.at[i], last_sem.at[0], peer_at(1 + i), False
+                        )
                 for i in range(2):
                     value = terms[side][i][c * half : (c + 1) * half]
                     value = value + relay_buf[side, i, strip].astype(F32)

time: 20.4 us -> 20.4 us (level)
  no operation moved by 1% of the time
where the time goes in v7:
time: 20.4 us; the launch traced here: 20.1 us
  Pallas kernels  19.5 us (96%)
  between operations  0.64 us (3%)
    pallas_call x1, Pallas kernels, pooled_call(): pl.pallas_call(functools.partial(pooled_kernel, micro, n_exp, n_dp), out_...  18.6 us
    pallas_call x1, Pallas kernels, settled(): pl.pallas_call(settle, out_shape=tuple((jax.ShapeDtypeStruct(a.shape, a.d...  0.91 us

profile of v7, /device:TPU:0, one launch (start us, length us, event | category | flops | bytes accessed | tf_op | source)
XLA Modules:
  0.0 20.1 jit_solution(1346399869507403543)
XLA Ops:
  0.6 18.6 %shard_map.102 = (bf16[256,1024]{1,0:T(8,128)(2,1)S(1)}, f32[128,256]{1,0:T(8,128)S(1)}, f32[128,256]{1,0:T(8,128)S(1)}, f32[128,256]{1,0:T(8,128)S(1)}) custom-call(s32[4,8,64]{2,1,0:T(8,128)} %bitcast.7, bf16[4,8,64]{2,1,0:T(8,128)(2,1)} %bitcast.8, bf16[256,1024]{1,0:T(8,128)(2,1)} %bitcast.5, bf16[4,4,8,1024]{3,2,1,0:T(8,128)(2,1)} %bitcast.6, ...), custom_call_target="tpu_custom_call" | custom-call | tf_op jit(solution)/shard_map/pallas_call | solution.py:716
  19.2 0.9 %shard_map.103 = (bf16[256,1024]{1,0:T(8,128)(2,1)}, f32[128,256]{1,0:T(8,128)}, f32[128,256]{1,0:T(8,128)}, f32[128,256]{1,0:T(8,128)}) custom-call(bf16[256,1024]{1,0:T(8,128)(2,1)S(1)} %get-tuple-element.12.refs_0_, f32[128,256]{1,0:T(8,128)S(1)} %get-tuple-element.13.refs_1_, f32[128,256]{1,0:T(8,128)S(1)} %get-tuple-element.14.refs_2_, ...), custom_call_target="tpu_custom_call" | custom-call | tf_op jit(solution)/shard_map/pallas_call | solution.py:692
